TPU v7x, 256 devices: a whole 4x4x8 slice. The times are simulated.
256 devices in a mesh: dp: 16 (over x, z_hi, core), seq: 16 (over z_lo, y).
Axes of the slice: x: 4, y: 4, z: 8 (z_hi: 2, z_lo: 4; z = z_hi * 4 + z_lo), core: 2. Of those that a mesh axis runs over, the one named last changes fastest.
Arguments:
- tokens: bfloat16 [32, 2304, 1280], P('dp', 'seq'), may hold values from -60 to 60
- pre_gain: float32 [1280], replicated, may hold values from 0.5 to 1.5
- pre_shift: float32 [1280], replicated, may hold values from -3 to 3
- w_qkv: bfloat16 [1280, 3840], P('dp'), may hold values from -4 to 4
- qkv_bias: float32 [3840], replicated, may hold values from -3 to 3
- w_out: bfloat16 [1280, 1280], P('dp'), may hold values from -0.15625 to 0.15625
- out_bias: float32 [1280], replicated, may hold values from -3 to 3
- mlp_gain: float32 [1280], replicated, may hold values from 0.5 to 1.5
- mlp_shift: float32 [1280], replicated, may hold values from -3 to 3
- w_up: bfloat16 [1280, 2560], P('dp'), may hold values from -0.15625 to 0.15625
- up_bias: float32 [2560], replicated, may hold values from -3 to 3
- w_down: bfloat16 [2560, 1280], P('dp'), may hold values from -0.125 to 0.125
- down_bias: float32 [1280], replicated, may hold values from -3 to 3
Outputs:
- layer_out: bfloat16 [32, 2304, 1280], P('dp', 'seq')
All inputs are finite; a program needn't handle non-finite values.
Results may differ from a plain program's by a relative error of at most 0.0039.
Values may be sent and summed in bfloat16 or wider, within the bound.
A program may use at most 128 MiB of HBM per device.

v0:
```python
import math
import jax
import jax.numpy as jnp
from jax import lax
from jax.sharding import PartitionSpec as P

HEADS = 16
HEAD_DIM = 80
EPSILON = 1e-05


def grouped_exchange(array, axis, split_dim, concat_dim, work, item_dim, out_dim):

    def moved(group):
        return lax.all_to_all(group, axis, split_axis=split_dim, concat_axis=concat_dim, tiled=True)

    items = jax.tree.leaves(array)[0].shape[item_dim]
    ends = [items * k // 2 for k in range(2 + 1)] if items % 2 == 0 else [0, items]
    groups = [
        jax.tree.map(lambda a: lax.slice_in_dim(a, low, high, axis=item_dim), array)
        for low, high in zip(ends, ends[1:])
    ]
    arrived = [moved(group) for group in groups]
    made = [work(group) for group in arrived]
    return jax.tree.map(lambda *parts: jnp.concatenate(parts, axis=out_dim), *made)


def normalize(features, gain, shift):
    average = jnp.mean(features, axis=-1, keepdims=True)
    centered = features - average
    spread = jnp.mean(centered * centered, axis=-1, keepdims=True)
    return centered * lax.rsqrt(spread + EPSILON) * gain + shift


def fold_rows(left_side, shard_piece):
    return jnp.dot(left_side, shard_piece, preferred_element_type=jnp.float32)


def query_block(length):
    block_rows = length
    while block_rows > 1024 and block_rows % 2 == 0:
        block_rows = block_rows // 2
    return block_rows


def attend_back(packed_items):
    count, length, heads_here, triple = packed_items.shape
    head_size = triple // 3
    block_rows = query_block(length)
    factor = 1.0 / math.sqrt(head_size)

    def one_picture(picture):
        key_rows = picture[:, :, head_size : 2 * head_size]
        value_rows = picture[:, :, 2 * head_size :]
        queries = picture[:, :, :head_size].reshape(
            length // block_rows, block_rows, heads_here, head_size
        )

        def one_block(query_rows):
            scores = (
                jnp.einsum("qhd,khd->hqk", query_rows, key_rows, preferred_element_type=jnp.float32)
                * factor
            )
            highest = jnp.max(scores, axis=-1, keepdims=True)
            weights = jnp.exp(scores - highest)
            probs = (weights / jnp.sum(weights, axis=-1, keepdims=True)).astype(jnp.bfloat16)
            mixed = jnp.einsum(
                "hqk,khd->qhd", probs, value_rows, preferred_element_type=jnp.float32
            )
            return mixed.astype(jnp.bfloat16)

        outputs = lax.map(one_block, queries)
        return outputs.reshape(length, heads_here * head_size)

    context = lax.map(one_picture, packed_items)
    return lax.all_to_all(context, "seq", split_axis=1, concat_axis=2, tiled=True)


def shards(
    tokens,
    pre_gain,
    pre_shift,
    w_qkv,
    qkv_bias,
    w_out,
    out_bias,
    mlp_gain,
    mlp_shift,
    w_up,
    up_bias,
    w_down,
    down_bias,
):
    images_here, tok_here, width = tokens.shape
    row_count = images_here * tok_here
    triple = 3 * HEAD_DIM
    residual = tokens.reshape(row_count, width).astype(jnp.float32)
    normed = normalize(residual, pre_gain, pre_shift).astype(jnp.bfloat16)
    projected = fold_rows(normed, lax.all_gather(w_qkv, "dp", axis=0, tiled=True))
    packed = (
        (projected + qkv_bias).astype(jnp.bfloat16).reshape(images_here, tok_here, HEADS, triple)
    )
    context = grouped_exchange(packed, "seq", 2, 1, attend_back, 0, 0)
    context = context.reshape(row_count, width)
    attended = fold_rows(context, lax.all_gather(w_out, "dp", axis=0, tiled=True))
    middle = residual + attended + out_bias
    normed_mlp = normalize(middle, mlp_gain, mlp_shift).astype(jnp.bfloat16)
    lifted = fold_rows(normed_mlp, lax.all_gather(w_up, "dp", axis=0, tiled=True))
    hidden = jax.nn.gelu(lifted + up_bias, approximate=False).astype(jnp.bfloat16)
    lowered = fold_rows(hidden, lax.all_gather(w_down, "dp", axis=0, tiled=True))
    result = (middle + lowered + down_bias).astype(jnp.bfloat16)
    return result.reshape(images_here, tok_here, width)


def solution(mesh):
    in_specs = (
        P("dp", "seq", None),
        P(),
        P(),
        P("dp", None),
        P(),
        P("dp", None),
        P(),
        P(),
        P(),
        P("dp", None),
        P(),
        P("dp", None),
        P(),
    )
    out_specs = P("dp", "seq", None)
    return jax.shard_map(shards, mesh=mesh, in_specs=in_specs, out_specs=out_specs, check_vma=False)
```

profile of v0, /device:TPU:1, one launch (start us, length us, event | category | flops | bytes accessed | tf_op | source)
XLA Modules:
  0.0 421.2 jit_solution(7809553857395419662)
XLA Ops:
  8.7 1.3 convert_reduce_fusion
  10.1 1.5 multiply_reduce_fusion.1
  11.7 1.1 fusion.37
  12.8 120.5 %all-gather.5.cloned.1.call-done = bf16[1280,3840]{1,0:T(8,128)(2,1)} async-done(((bf16[80,3840]{1,0:T(8,128)(2,1)}), bf16[1280,3840]{1,0:T(8,128)(2,1)}) %all-gather.5.cloned.1.call-update) | async-done | bytes 9830416 | tf_op jit(solution)/shard_map/all_gather | solution.py:99
  133.3 7.1 %fusion.20 = bf16[288,3840]{1,0:T(8,128)(2,1)S(1)} fusion(bf16[288,1280]{1,0:T(8,128)(2,1)S(1)} %fusion.37, bf16[1280,3840]{1,0:T(8,128)(2,1)} %all-gather.5.cloned.1.call-done, f32[3840]{0:T(1024)S(1)} %copy-done.1), kind=kOutput, calls=%fused_computation.27 | convolution fusion | flops 2833367040 | bytes 12794880 | tf_op jit(solution)/shard_map/dot_general | solution.py:36
  140.3 1.1 fusion.109
  141.5 2.8 slice.37
  144.3 1.5 copy.40
  145.8 4.1 all-to-all-start
  150.5 3.7 slice.42
  154.1 1.4 copy.48
  155.6 20.2 %all-to-all-done = bf16[1,144,16,240]{3,1,0,2:T(8,128)(2,1)S(1)} async-done(((bf16[1,144,16,240]{3,1,0,2:T(8,128)(2,1)}), bf16[1,144,16,240]{3,1,0,2:T(8,128)(2,1)S(1)}, u32[]{:S(2)}, u32[]{:S(2)}) %all-to-all-start) | async-done | bytes 1105952 | tf_op jit(solution)/shard_map/all_to_all | solution.py:15
  175.8 26.0 %all-to-all-start.2 = ((bf16[1,144,16,240]{3,1,0,2:T(8,128)(2,1)}), bf16[1,144,16,240]{3,1,0,2:T(8,128)(2,1)S(1)}, u32[]{:S(2)}, u32[]{:S(2)}) async-start(bf16[1,144,16,240]{3,1,0,2:T(8,128)(2,1)} %copy.48), calls=%async_computation.2 | async-start | bytes 2359296 | tf_op jit(solution)/shard_map/all_to_all | solution.py:15
  201.9 1.6 fusion.110
  203.5 1.3 copy.41
  204.8 1.3 copy.42
  206.1 1.3 copy.43
  207.5 12.2 %while.34 = (s32[]{:T(128)}, bf16[4,576,1,80]{1,3,2,0:T(8,128)(2,1)S(1)}, bf16[4,576,1,80]{1,3,2,0:T(8,128)(2,1)S(1)}, bf16[2304,1,80]{0,2,1:T(8,128)(2,1)S(1)}, bf16[2304,1,80]{0,2,1:T(8,128)(2,1)S(1)}, /*index=5*/s32[]{:T(128)}) while((s32[]{:T(128)}, bf16[4,576,1,80]{1,3,2,0:T(8,128)(2,1)S(1)}, bf16[4,576,1,80]{1,3,2,0:T(8,128)(2,1)S(1)}, ...), condition=%wide.region_5.0_spmd, body=%wide.region_2.5_spmd.sunk | while | flops 434007936 | bytes 16882508 | solution.py:72
  209.3 1.2 fusion.130
  212.4 1.2 fusion.130
  215.4 1.2 fusion.130
  218.4 1.2 fusion.130
  219.6 1.1 copy.56
  220.7 3.5 reshape.145
  224.7 13.6 %reduce.11 = bf16[2304,80]{1,0:T(8,128)(2,1)} reduce(bf16[2304,1,80]{2,1,0:T(2,128)(2,1)S(1)} %bitcast.118, bf16[]{:T(256)} %broadcast.108), dimensions={1}, to_apply=%bitcast.83.reduce_sub_computation | reduce | bytes 737282
  238.3 2.8 reshape.149
  241.1 7.2 %all-to-all-start.1 = ((bf16[16,2,5760]{2,1,0:T(2,128)(2,1)}), bf16[16,2,5760]{2,1,0:T(2,128)(2,1)S(1)}, u32[]{:S(2)}, u32[]{:S(2)}) async-start(bf16[16,2,5760]{2,1,0:T(2,128)(2,1)} %reshape.149), calls=%async_computation.1 | async-start | bytes 737280 | tf_op jit(solution)/shard_map/all_to_all | solution.py:76
  248.4 1.3 fusion.111
  249.6 1.3 copy.49
  251.5 12.2 %while.35 = (s32[]{:T(128)}, bf16[4,576,1,80]{1,3,2,0:T(8,128)(2,1)S(1)}, bf16[4,576,1,80]{1,3,2,0:T(8,128)(2,1)S(1)}, bf16[2304,1,80]{0,2,1:T(8,128)(2,1)S(1)}, bf16[2304,1,80]{0,2,1:T(8,128)(2,1)S(1)}, /*index=5*/s32[]{:T(128)}) while((s32[]{:T(128)}, bf16[4,576,1,80]{1,3,2,0:T(8,128)(2,1)S(1)}, bf16[4,576,1,80]{1,3,2,0:T(8,128)(2,1)S(1)}, ...), condition=%wide.region_9.10_spmd, body=%wide.region_6.0_spmd.sunk | while | flops 434007936 | bytes 16882508 | solution.py:72
  253.3 1.2 fusion.134
  256.4 1.2 fusion.134
  259.4 1.2 fusion.134
  262.4 1.2 fusion.134
  264.2 12.8 %reduce.10 = bf16[2304,80]{1,0:T(8,128)(2,1)S(1)} reduce(bf16[2304,1,80]{2,1,0:T(2,128)(2,1)S(1)} %bitcast.119, bf16[]{:T(256)} %broadcast.108), dimensions={1}, to_apply=%bitcast.81.reduce_sub_computation | reduce | bytes 737282
  277.0 1.8 reshape.147
  278.8 20.5 %all-to-all-start.3 = ((bf16[16,2,5760]{2,1,0:T(2,128)(2,1)}), bf16[16,2,5760]{2,1,0:T(2,128)(2,1)S(1)}, u32[]{:S(2)}, u32[]{:S(2)}) async-start(bf16[16,2,5760]{2,1,0:T(2,128)(2,1)} %reshape.147), calls=%async_computation.3 | async-start | bytes 737280 | tf_op jit(solution)/shard_map/all_to_all | solution.py:76
  299.3 1.3 reshape.150
  300.6 1.5 copy.46
  302.1 1.1 all_to_all.52
  304.8 5.7 %all-to-all-done.3 = bf16[16,2,5760]{2,1,0:T(2,128)(2,1)S(1)} async-done(((bf16[16,2,5760]{2,1,0:T(2,128)(2,1)}), bf16[16,2,5760]{2,1,0:T(2,128)(2,1)S(1)}, u32[]{:S(2)}, u32[]{:S(2)}) %all-to-all-start.3) | async-done | bytes 368672 | tf_op jit(solution)/shard_map/all_to_all | solution.py:76
  310.5 1.3 reshape.148
  311.7 1.7 copy.54
  313.4 1.1 all_to_all.59
  314.6 1.0 copy.55
  316.3 3.4 fusion.112
  320.0 79.5 %all-gather.9.cloned.1.call-done = bf16[1280,2560]{1,0:T(8,128)(2,1)} async-done(((bf16[80,2560]{1,0:T(8,128)(2,1)}), bf16[1280,2560]{1,0:T(8,128)(2,1)}) %all-gather.9.cloned.1.call-update) | async-done | bytes 6553616 | tf_op jit(solution)/shard_map/all_gather | solution.py:108
  399.5 14.9 %fusion.33 = bf16[288,1280]{1,0:T(8,128)(2,1)} fusion(f32[288,1280]{1,0:T(8,128)S(1)} %get-tuple-element.142, bf16[2560,1280]{1,0:T(8,128)(2,1)} %all-gather.11.cloned.1.call-done, bf16[1280,2560]{1,0:T(8,128)(2,1)} %all-gather.9.cloned.1.call-done, f32[2560]{0:T(1024)S(1)} %copy-done.2, f32[1280]{0:T(1024)S(1)} %copy-done.4, f32[1280]{0:T(1024)S(1)} %copy-done.5, ...), kind=kOutput, calls=%fused_computation.52 | convolution fusion | flops 3826483200 | bytes 15346944 | tf_op jit(solution)/shard_map/dot_general | solution.py:36
  (60 shorter events, 21.9 us)
Async XLA Ops:
  6.5 5.1 %copy-start = (bf16[2,144,1280]{2,1,0:T(8,128)(2,1)S(1)}, bf16[2,144,1280]{2,1,0:T(8,128)(2,1)}, u32[]{:S(2)}) copy-start(bf16[2,144,1280]{2,1,0:T(8,128)(2,1)} %param.17) | copy-start | bytes 2211844
  6.5 126.7 %copy-start.1 = (f32[3840]{0:T(1024)S(1)}, f32[3840]{0:T(1024)}, u32[]{:S(2)}) copy-start(f32[3840]{0:T(1024)} %param.21) | copy-start | bytes 46084
  6.5 126.7 %all-gather.5.cloned.1.call-start = ((), (), s32[]{:S(2)}) async-start(), calls=%async_computation.4 | async-start | bytes 10444800 | tf_op jit(solution)/shard_map/all_gather | solution.py:99
  7.3 309.0 %all-gather.7.cloned.1.call-start = ((), (), s32[]{:S(2)}) async-start(), calls=%async_computation.5 | async-start | bytes 3481600 | tf_op jit(solution)/shard_map/all_gather | solution.py:105
  8.0 312.0 %all-gather.11.cloned.1.call-start = ((), (), s32[]{:S(2)}) async-start(), calls=%async_computation.7 | async-start | bytes 6963200 | tf_op jit(solution)/shard_map/all_gather | solution.py:110
  145.8 30.0 %all-to-all-start = ((bf16[1,144,16,240]{3,1,0,2:T(8,128)(2,1)}), bf16[1,144,16,240]{3,1,0,2:T(8,128)(2,1)S(1)}, u32[]{:S(2)}, u32[]{:S(2)}) async-start(bf16[1,144,16,240]{3,1,0,2:T(8,128)(2,1)} %copy.40), calls=%async_computation | async-start | bytes 2359296 | tf_op jit(solution)/shard_map/all_to_all | solution.py:15
  149.9 249.6 %all-gather.9.cloned.1.call-start = ((), (), s32[]{:S(2)}) async-start(), calls=%async_computation.6 | async-start | bytes 6963200 | tf_op jit(solution)/shard_map/all_gather | solution.py:108
  175.8 65.3 %all-to-all-start.2 = ((bf16[1,144,16,240]{3,1,0,2:T(8,128)(2,1)}), bf16[1,144,16,240]{3,1,0,2:T(8,128)(2,1)S(1)}, u32[]{:S(2)}, u32[]{:S(2)}) async-start(bf16[1,144,16,240]{3,1,0,2:T(8,128)(2,1)} %copy.48), calls=%async_computation.2 | async-start | bytes 2359296 | tf_op jit(solution)/shard_map/all_to_all | solution.py:15
  241.1 37.7 %all-to-all-start.1 = ((bf16[16,2,5760]{2,1,0:T(2,128)(2,1)}), bf16[16,2,5760]{2,1,0:T(2,128)(2,1)S(1)}, u32[]{:S(2)}, u32[]{:S(2)}) async-start(bf16[16,2,5760]{2,1,0:T(2,128)(2,1)} %reshape.149), calls=%async_computation.1 | async-start | bytes 737280 | tf_op jit(solution)/shard_map/all_to_all | solution.py:76
  278.8 31.6 %all-to-all-start.3 = ((bf16[16,2,5760]{2,1,0:T(2,128)(2,1)}), bf16[16,2,5760]{2,1,0:T(2,128)(2,1)S(1)}, u32[]{:S(2)}, u32[]{:S(2)}) async-start(bf16[16,2,5760]{2,1,0:T(2,128)(2,1)} %reshape.147), calls=%async_computation.3 | async-start | bytes 737280 | tf_op jit(solution)/shard_map/all_to_all | solution.py:76
  311.7 4.5 %copy-start.3 = (f32[1280]{0:T(1024)S(1)}, f32[1280]{0:T(1024)}, u32[]{:S(2)}) copy-start(f32[1280]{0:T(1024)} %param.23) | copy-start | bytes 15364
  316.3 83.2 %copy-start.2 = (f32[2560]{0:T(1024)S(1)}, f32[2560]{0:T(1024)}, u32[]{:S(2)}) copy-start(f32[2560]{0:T(1024)} %param.27) | copy-start | bytes 30724
  316.3 83.2 %copy-start.4 = (f32[1280]{0:T(1024)S(1)}, f32[1280]{0:T(1024)}, u32[]{:S(2)}) copy-start(f32[1280]{0:T(1024)} %param.29) | copy-start | bytes 15364
  316.3 83.2 %copy-start.5 = (f32[1280]{0:T(1024)S(1)}, f32[1280]{0:T(1024)}, u32[]{:S(2)}) copy-start(f32[1280]{0:T(1024)} %param.25) | copy-start | bytes 15364
  316.3 83.2 %copy-start.6 = (f32[1280]{0:T(1024)S(1)}, f32[1280]{0:T(1024)}, u32[]{:S(2)}) copy-start(f32[1280]{0:T(1024)} %param.24) | copy-start | bytes 15364
Sparse Core Ops, SparseCore 0:
  10.0 123.1 all-gather.4
  135.9 59.7 all-gather.6
  198.5 104.8 all-gather.10
  305.9 93.5 all-gather.8
where the time goes:
time: 427 us; the launch traced here: 421 us
  waiting for transfers between devices  229 us (54%)
  starting transfers between devices  58 us (14%)
  matrix products  42.6 us (10%)
  local copies, waits for them, and re-layouts  40.7 us (10%)
  other arithmetic  37.5 us (9%)
  between operations  13.7 us (3%)
    all_gather x1, waiting for transfers between devices, shards(): lax.all_gather(w_qkv, 'dp', axis=0, tiled=True)  120 us
    all_gather x1, waiting for transfers between devices, shards(): lax.all_gather(w_up, 'dp', axis=0, tiled=True)  79.5 us
    all_to_all x2, starting transfers between devices, moved(): lax.all_to_all(group, axis, split_axis=split_dim, concat_axis=concat_dim,...  30.2 us
    all_to_all x2, starting transfers between devices, attend_back(): lax.all_to_all(context, 'seq', split_axis=1, concat_axis=2, tiled=True)  27.7 us
    unnamed x2, other arithmetic  26.4 us
    dot_general x3, matrix products, fold_rows(): return jnp.dot(left_side, shard_piece, preferred_element_type=jnp.float32)  25.4 us
    all_to_all x2, waiting for transfers between devices, moved(): lax.all_to_all(group, axis, split_axis=split_dim, concat_axis=concat_dim,...  20.3 us
    slice x5, local copies, waits for them, and re-layouts, grouped_exchange(): lax.slice_in_dim(a, low, high, axis=item_dim)  10.5 us
  transfers between devices with their start and end apart: 8, of which 4 were waited for; matrix products, arithmetic and copies ran while one was open for 24% of the time, Pallas kernels for 0%

commit v1 on v0

--- a/solution.py
+++ b/solution.py
@@ -105,7 +105,12 @@
     attended = fold_rows(context, lax.all_gather(w_out, "dp", axis=0, tiled=True))
     middle = residual + attended + out_bias
     normed_mlp = normalize(middle, mlp_gain, mlp_shift).astype(jnp.bfloat16)
-    lifted = fold_rows(normed_mlp, lax.all_gather(w_up, "dp", axis=0, tiled=True))
+    lifted = fold_rows(
+        normed_mlp,
+        jnp.concatenate(
+            lax.all_to_all(jnp.stack([w_up] * lax.axis_size("dp")), "dp", 0, 0), axis=0
+        ),
+    )
     hidden = jax.nn.gelu(lifted + up_bias, approximate=False).astype(jnp.bfloat16)
     lowered = fold_rows(hidden, lax.all_gather(w_down, "dp", axis=0, tiled=True))
     result = (middle + lowered + down_bias).astype(jnp.bfloat16)

time: 427 us -> 534 us (1.25)
  waiting for transfers between devices: 229 us -> 355 us
  starting transfers between devices: 58 us -> 29.5 us
  blocking collectives: 0 us -> 16.7 us
  local copies, waits for them, and re-layouts: 40.7 us -> 33.1 us
    all_gather x1, waiting for transfers between devices: 0.02 us -> 106 us  [shards(): lax.all_gather(w_down, 'dp', axis=0, tiled=True)]
    all_to_all x0 -> x1, waiting for transfers between devices: none -> 89.3 us  [shards(): lax.all_to_all(jnp.stack([w_up] * lax.axis_size('dp')), 'dp', 0, 0)]
    all_gather x1 -> x0, waiting for transfers between devices: 79.5 us -> none  [shards(): lax.all_gather(w_up, 'dp', axis=0, tiled=True)]
    all_to_all x2 -> x1, starting transfers between devices: 27.7 us -> 8.56 us  [attend_back(): lax.all_to_all(context, 'seq', split_axis=1, concat_axis=2, tiled=True)]
    all_to_all x2, starting transfers between devices: 30.2 us -> 12.7 us  [moved(): lax.all_to_all(group, axis, split_axis=split_dim, concat_axis=concat_dim,...]
    all_to_all x0 -> x1, blocking collectives: none -> 16.7 us  [attend_back(): lax.all_to_all(context, 'seq', split_axis=1, concat_axis=2, tiled=True)]
    all_to_all x2, waiting for transfers between devices: 20.3 us -> 35.1 us  [moved(): lax.all_to_all(group, axis, split_axis=split_dim, concat_axis=concat_dim,...]
    all_to_all x0 -> x1, starting transfers between devices: none -> 8.17 us  [shards(): lax.all_to_all(jnp.stack([w_up] * lax.axis_size('dp')), 'dp', 0, 0)]
  transfers between devices with their start and end apart: 8 -> 7, of which waited for: 4 -> 5; matrix products, arithmetic and copies ran while one was open for 24% -> 16% of each run, Pallas kernels for 0% -> 0%
where the time goes in v1:
time: 534 us; the launch traced here: 527 us
  waiting for transfers between devices  355 us (66%)
  matrix products  42.3 us (8%)
  other arithmetic  37.3 us (7%)
  local copies, waits for them, and re-layouts  33.1 us (6%)
  starting transfers between devices  29.5 us (6%)
  blocking collectives  16.7 us (3%)
  between operations  13.7 us (3%)
    all_gather x1, waiting for transfers between devices, shards(): lax.all_gather(w_qkv, 'dp', axis=0, tiled=True)  122 us
    all_gather x1, waiting for transfers between devices, shards(): lax.all_gather(w_down, 'dp', axis=0, tiled=True)  106 us
    all_to_all x1, waiting for transfers between devices, shards(): lax.all_to_all(jnp.stack([w_up] * lax.axis_size('dp')), 'dp', 0, 0)  89.3 us
    all_to_all x2, waiting for transfers between devices, moved(): lax.all_to_all(group, axis, split_axis=split_dim, concat_axis=concat_dim,...  35.1 us
    unnamed x2, other arithmetic  25.8 us
    dot_general x3, matrix products, fold_rows(): return jnp.dot(left_side, shard_piece, preferred_element_type=jnp.float32)  25.2 us
    all_to_all x1, blocking collectives, attend_back(): lax.all_to_all(context, 'seq', split_axis=1, concat_axis=2, tiled=True)  16.7 us
    all_to_all x2, starting transfers between devices, moved(): lax.all_to_all(group, axis, split_axis=split_dim, concat_axis=concat_dim,...  12.7 us
  transfers between devices with their start and end apart: 7, of which 5 were waited for; matrix products, arithmetic and copies ran while one was open for 16% of the time, Pallas kernels for 0%

profile of v1, /device:TPU:1, one launch (start us, length us, event | category | flops | bytes accessed | tf_op | source)
XLA Modules:
  0.0 527.3 jit_solution(3434268846761647090)
XLA Ops:
  7.3 1.3 convert_reduce_fusion
  8.6 1.5 multiply_reduce_fusion.1
  10.2 1.5 fusion.37
  11.7 121.6 %all-gather.4.cloned.1.call-done = bf16[1280,3840]{1,0:T(8,128)(2,1)} async-done(((bf16[80,3840]{1,0:T(8,128)(2,1)}), bf16[1280,3840]{1,0:T(8,128)(2,1)}) %all-gather.4.cloned.1.call-update) | async-done | bytes 9830416 | tf_op jit(solution)/shard_map/all_gather | solution.py:99
  133.2 7.1 %fusion.20 = bf16[288,3840]{1,0:T(8,128)(2,1)S(1)} fusion(bf16[288,1280]{1,0:T(8,128)(2,1)S(1)} %fusion.37, bf16[1280,3840]{1,0:T(8,128)(2,1)} %all-gather.4.cloned.1.call-done, f32[3840]{0:T(1024)S(1)} %copy-done.1), kind=kOutput, calls=%fused_computation.27 | convolution fusion | flops 2833367040 | bytes 12794880 | tf_op jit(solution)/shard_map/dot_general | solution.py:36
  140.5 2.8 slice.37
  143.3 1.4 copy.40
  144.7 4.1 all-to-all-start
  149.6 2.8 slice.42
  152.4 1.4 copy.48
  153.8 24.3 %all-to-all-done = bf16[1,144,16,240]{3,1,0,2:T(8,128)(2,1)S(1)} async-done(((bf16[1,144,16,240]{3,1,0,2:T(8,128)(2,1)}), bf16[1,144,16,240]{3,1,0,2:T(8,128)(2,1)S(1)}, u32[]{:S(2)}, u32[]{:S(2)}) %all-to-all-start) | async-done | bytes 1105952 | tf_op jit(solution)/shard_map/all_to_all | solution.py:15
  178.1 8.6 %all-to-all-start.2 = ((bf16[1,144,16,240]{3,1,0,2:T(8,128)(2,1)}), bf16[1,144,16,240]{3,1,0,2:T(8,128)(2,1)S(1)}, u32[]{:S(2)}, u32[]{:S(2)}) async-start(bf16[1,144,16,240]{3,1,0,2:T(8,128)(2,1)} %copy.48), calls=%async_computation.2 | async-start | bytes 2359296 | tf_op jit(solution)/shard_map/all_to_all | solution.py:15
  186.7 1.3 fusion.110
  187.9 1.3 copy.41
  189.8 12.1 %while.34 = (s32[]{:T(128)}, bf16[4,576,1,80]{1,3,2,0:T(8,128)(2,1)S(1)}, bf16[4,576,1,80]{1,3,2,0:T(8,128)(2,1)S(1)}, bf16[2304,1,80]{0,2,1:T(8,128)(2,1)S(1)}, bf16[2304,1,80]{0,2,1:T(8,128)(2,1)S(1)}, /*index=5*/s32[]{:T(128)}) while((s32[]{:T(128)}, bf16[4,576,1,80]{1,3,2,0:T(8,128)(2,1)S(1)}, bf16[4,576,1,80]{1,3,2,0:T(8,128)(2,1)S(1)}, ...), condition=%wide.region_5.0_spmd, body=%wide.region_2.5_spmd.sunk | while | flops 434007936 | bytes 16882508 | solution.py:72
  191.7 1.2 fusion.130
  194.7 1.2 fusion.130
  197.7 1.2 fusion.130
  198.9 1.0 fusion.128
  200.7 1.2 fusion.130
  203.0 12.9 %reduce.11 = bf16[2304,80]{1,0:T(8,128)(2,1)S(1)} reduce(bf16[2304,1,80]{2,1,0:T(2,128)(2,1)S(1)} %bitcast.119, bf16[]{:T(256)} %broadcast.110), dimensions={1}, to_apply=%bitcast.84.reduce_sub_computation | reduce | bytes 737282
  215.9 1.8 reshape.155
  217.7 10.9 %all-to-all-done.2 = bf16[1,144,16,240]{3,1,0,2:T(8,128)(2,1)S(1)} async-done(((bf16[1,144,16,240]{3,1,0,2:T(8,128)(2,1)}), bf16[1,144,16,240]{3,1,0,2:T(8,128)(2,1)S(1)}, u32[]{:S(2)}, u32[]{:S(2)}) %all-to-all-start.2) | async-done | bytes 1105952 | tf_op jit(solution)/shard_map/all_to_all | solution.py:15
  228.6 8.6 %all-to-all-start.1 = ((bf16[16,2,5760]{2,1,0:T(2,128)(2,1)}), bf16[16,2,5760]{2,1,0:T(2,128)(2,1)S(1)}, u32[]{:S(2)}, u32[]{:S(2)}) async-start(bf16[16,2,5760]{2,1,0:T(2,128)(2,1)} %reshape.155), calls=%async_computation.1 | async-start | bytes 737280 | tf_op jit(solution)/shard_map/all_to_all | solution.py:76
  238.4 12.2 %while.35 = (s32[]{:T(128)}, bf16[4,576,1,80]{1,3,2,0:T(8,128)(2,1)S(1)}, bf16[4,576,1,80]{1,3,2,0:T(8,128)(2,1)S(1)}, bf16[2304,1,80]{0,2,1:T(8,128)(2,1)S(1)}, bf16[2304,1,80]{0,2,1:T(8,128)(2,1)S(1)}, /*index=5*/s32[]{:T(128)}) while((s32[]{:T(128)}, bf16[4,576,1,80]{1,3,2,0:T(8,128)(2,1)S(1)}, bf16[4,576,1,80]{1,3,2,0:T(8,128)(2,1)S(1)}, ...), condition=%wide.region_9.10_spmd, body=%wide.region_6.0_spmd.sunk | while | flops 434007936 | bytes 16882508 | solution.py:72
  240.2 1.2 fusion.134
  241.4 1.0 fusion.132
  243.3 1.2 fusion.134
  246.3 1.2 fusion.134
  247.5 1.0 fusion.132
  249.4 1.2 fusion.134
  251.1 12.9 %reduce.10 = bf16[2304,80]{1,0:T(8,128)(2,1)S(1)} reduce(bf16[2304,1,80]{2,1,0:T(2,128)(2,1)S(1)} %bitcast.120, bf16[]{:T(256)} %broadcast.110), dimensions={1}, to_apply=%bitcast.82.reduce_sub_computation | reduce | bytes 737282
  264.0 1.1 reshape.153
  265.1 16.7 %all_to_all.71 = bf16[16,2,5760]{2,1,0:T(2,128)(2,1)S(1)} all-to-all(bf16[16,2,5760]{2,1,0:T(2,128)(2,1)S(1)} %reshape.153), channel_id=1, replica_groups=mesh['dp'=16,'seq'=16] {'seq'}, dimensions={0} | all-to-all | bytes 737280 | tf_op jit(solution)/shard_map/all_to_all | solution.py:76
  281.8 4.3 stack.2
  286.1 8.2 %all-to-all-start.4 = ((bf16[16,80,2560]{2,1,0:T(8,128)(2,1)}), bf16[16,80,2560]{2,1,0:T(8,128)(2,1)}, u32[]{:S(2)}, u32[]{:S(2)}) async-start(bf16[16,80,2560]{2,1,0:T(8,128)(2,1)} %stack.2), calls=%async_computation.4 | async-start | bytes 13107200 | tf_op jit(solution)/shard_map/all_to_all | solution.py:111
  295.0 1.3 reshape.156
  296.3 1.5 copy.46
  297.8 1.1 all_to_all.55
  298.9 1.0 copy.47
  300.5 1.3 reshape.154
  301.8 1.7 copy.54
  303.5 1.1 all_to_all.62
  304.6 1.0 copy.55
  306.4 3.2 fusion.112
  309.9 89.3 %all-to-all-done.4 = bf16[16,80,2560]{2,1,0:T(8,128)(2,1)} async-done(((bf16[16,80,2560]{2,1,0:T(8,128)(2,1)}), bf16[16,80,2560]{2,1,0:T(8,128)(2,1)}, u32[]{:S(2)}, u32[]{:S(2)}) %all-to-all-start.4) | async-done | bytes 6553632 | tf_op jit(solution)/shard_map/all_to_all | solution.py:111
  399.2 106.4 %all-gather.8.cloned.1.call-done = bf16[2560,1280]{1,0:T(8,128)(2,1)} async-done(((bf16[160,1280]{1,0:T(8,128)(2,1)}), bf16[2560,1280]{1,0:T(8,128)(2,1)}) %all-gather.8.cloned.1.call-update) | async-done | bytes 6553616 | tf_op jit(solution)/shard_map/all_gather | solution.py:115
  505.6 14.9 %fusion.33 = bf16[288,1280]{1,0:T(8,128)(2,1)} fusion(f32[288,1280]{1,0:T(8,128)S(1)} %get-tuple-element.142, bf16[2560,1280]{1,0:T(8,128)(2,1)} %all-gather.8.cloned.1.call-done, bf16[1280,2560]{1,0:T(8,128)(2,1)} %bitcast.30, f32[2560]{0:T(1024)S(1)} %copy-done.2, f32[1280]{0:T(1024)S(1)} %copy-done.4, f32[1280]{0:T(1024)S(1)} %copy-done.5, ...), kind=kOutput, calls=%fused_computation.52 | convolution fusion | flops 3826483200 | bytes 15346944 | tf_op jit(solution)/shard_map/dot_general | solution.py:36
  (59 shorter events, 19.3 us)
Async XLA Ops:
  6.5 126.7 %copy-start.1 = (f32[3840]{0:T(1024)S(1)}, f32[3840]{0:T(1024)}, u32[]{:S(2)}) copy-start(f32[3840]{0:T(1024)} %param.21) | copy-start | bytes 46084
  6.5 126.7 %all-gather.4.cloned.1.call-start = ((), (), s32[]{:S(2)}) async-start(), calls=%async_computation.5 | async-start | bytes 10444800 | tf_op jit(solution)/shard_map/all_gather | solution.py:99
  144.7 33.4 %all-to-all-start = ((bf16[1,144,16,240]{3,1,0,2:T(8,128)(2,1)}), bf16[1,144,16,240]{3,1,0,2:T(8,128)(2,1)S(1)}, u32[]{:S(2)}, u32[]{:S(2)}) async-start(bf16[1,144,16,240]{3,1,0,2:T(8,128)(2,1)} %copy.40), calls=%async_computation | async-start | bytes 2359296 | tf_op jit(solution)/shard_map/all_to_all | solution.py:15
  148.8 157.4 %all-gather.6.cloned.1.call-start = ((), (), s32[]{:S(2)}) async-start(), calls=%async_computation.6 | async-start | bytes 3481600 | tf_op jit(solution)/shard_map/all_gather | solution.py:105
  178.1 50.5 %all-to-all-start.2 = ((bf16[1,144,16,240]{3,1,0,2:T(8,128)(2,1)}), bf16[1,144,16,240]{3,1,0,2:T(8,128)(2,1)S(1)}, u32[]{:S(2)}, u32[]{:S(2)}) async-start(bf16[1,144,16,240]{3,1,0,2:T(8,128)(2,1)} %copy.48), calls=%async_computation.2 | async-start | bytes 2359296 | tf_op jit(solution)/shard_map/all_to_all | solution.py:15
  228.6 36.5 %all-to-all-start.1 = ((bf16[16,2,5760]{2,1,0:T(2,128)(2,1)}), bf16[16,2,5760]{2,1,0:T(2,128)(2,1)S(1)}, u32[]{:S(2)}, u32[]{:S(2)}) async-start(bf16[16,2,5760]{2,1,0:T(2,128)(2,1)} %reshape.155), calls=%async_computation.1 | async-start | bytes 737280 | tf_op jit(solution)/shard_map/all_to_all | solution.py:76
  286.1 113.1 %all-to-all-start.4 = ((bf16[16,80,2560]{2,1,0:T(8,128)(2,1)}), bf16[16,80,2560]{2,1,0:T(8,128)(2,1)}, u32[]{:S(2)}, u32[]{:S(2)}) async-start(bf16[16,80,2560]{2,1,0:T(8,128)(2,1)} %stack.2), calls=%async_computation.4 | async-start | bytes 13107200 | tf_op jit(solution)/shard_map/all_to_all | solution.py:111
  294.3 211.3 %all-gather.8.cloned.1.call-start = ((), (), s32[]{:S(2)}) async-start(), calls=%async_computation.7 | async-start | bytes 6963200 | tf_op jit(solution)/shard_map/all_gather | solution.py:115
  301.8 4.5 copy-start
  301.8 4.5 copy-start.3
  306.3 199.3 %copy-start.2 = (f32[2560]{0:T(1024)S(1)}, f32[2560]{0:T(1024)}, u32[]{:S(2)}) copy-start(f32[2560]{0:T(1024)} %param.27) | copy-start | bytes 30724
  306.3 199.3 %copy-start.4 = (f32[1280]{0:T(1024)S(1)}, f32[1280]{0:T(1024)}, u32[]{:S(2)}) copy-start(f32[1280]{0:T(1024)} %param.29) | copy-start | bytes 15364
  306.3 199.3 %copy-start.5 = (f32[1280]{0:T(1024)S(1)}, f32[1280]{0:T(1024)}, u32[]{:S(2)}) copy-start(f32[1280]{0:T(1024)} %param.25) | copy-start | bytes 15364
  306.4 199.2 %copy-start.6 = (f32[1280]{0:T(1024)S(1)}, f32[1280]{0:T(1024)}, u32[]{:S(2)}) copy-start(f32[1280]{0:T(1024)} %param.24) | copy-start | bytes 15364
Sparse Core Ops, SparseCore 0:
  10.0 123.1 all-gather.3
  152.3 79.1 all-gather.5
  297.8 207.7 all-gather.7
